TPU v7x, 32 devices: a whole 2x2x4 slice. The times are simulated.
32 devices in a mesh: dp: 16 (over z, x, core), blk: 2 (over y).
Axes of the slice: x: 2, y: 2, z: 4, core: 2. Of those that a mesh axis runs over, the one named last changes fastest.
Arguments:
- patches: bfloat16 [16, 1024, 768], P('dp', 'blk'), may hold values from -6 to 6
- vis_slot: int32 [16, 1024], P('dp', 'blk'), may hold values from 0 to 671, as said below
- seg_ids: int32 [16, 1344], P('dp', 'blk'), may hold values from 0 to 5, never falling along the last dimension, each value on 1 to 840 neighbouring positions
- enc_norm1_gain: bfloat16 [768], replicated, may hold values from 0.25 to 1.75
- enc_norm1_bias: bfloat16 [768], replicated, may hold values from -1.75 to 1.75
- enc_qkv_weight: bfloat16 [768, 2304], replicated, may hold values from -0.21875 to 0.21875
- enc_query_bias: bfloat16 [768], replicated, may hold values from -3 to 3
- enc_value_bias: bfloat16 [768], replicated, may hold values from -3 to 3
- enc_out_weight: bfloat16 [768, 768], replicated, may hold values from -0.875 to 0.875
- enc_out_bias: bfloat16 [768], replicated, may hold values from -1.75 to 1.75
- enc_norm2_gain: bfloat16 [768], replicated, may hold values from 0.25 to 1.75
- enc_norm2_bias: bfloat16 [768], replicated, may hold values from -1.75 to 1.75
- enc_up_weight: bfloat16 [768, 3072], replicated, may hold values from -0.21875 to 0.21875
- enc_up_bias: bfloat16 [3072], replicated, may hold values from -3 to 3
- enc_down_weight: bfloat16 [3072, 768], replicated, may hold values from -0.109375 to 0.109375
- enc_down_bias: bfloat16 [768], replicated, may hold values from -1.75 to 1.75
- emb_weight: bfloat16 [768, 512], replicated, may hold values from -0.21875 to 0.21875
- emb_bias: bfloat16 [512], replicated, may hold values from -3 to 3
- mask_token: bfloat16 [512], replicated, may hold values from -6 to 6
- dec_norm1_gain: bfloat16 [512], replicated, may hold values from 0.25 to 1.75
- dec_norm1_bias: bfloat16 [512], replicated, may hold values from -1.75 to 1.75
- dec_qkv_weight: bfloat16 [512, 1536], replicated, may hold values from -0.25 to 0.25
- dec_query_bias: bfloat16 [512], replicated, may hold values from -3 to 3
- dec_value_bias: bfloat16 [512], replicated, may hold values from -3 to 3
- dec_out_weight: bfloat16 [512, 512], replicated, may hold values from -1 to 1
- dec_out_bias: bfloat16 [512], replicated, may hold values from -3.5 to 3.5
- dec_norm2_gain: bfloat16 [512], replicated, may hold values from 0.25 to 1.75
- dec_norm2_bias: bfloat16 [512], replicated, may hold values from -1.75 to 1.75
- dec_up_weight: bfloat16 [512, 2048], replicated, may hold values from -0.25 to 0.25
- dec_up_bias: bfloat16 [2048], replicated, may hold values from -3 to 3
- dec_down_weight: bfloat16 [2048, 512], replicated, may hold values from -0.125 to 0.125
- dec_down_bias: bfloat16 [512], replicated, may hold values from -6 to 6
- cotangent: bfloat16 [16, 1344, 512], P('dp', 'blk'), may hold values from -6 to 6
Outputs:
- dec_out: bfloat16 [16, 1344, 512], P('dp', 'blk')
- grad_patches: bfloat16 [16, 1024, 768], P('dp', 'blk')
- grad_enc_norm1_gain: float32 [768], P('dp')
- grad_enc_norm1_bias: float32 [768], P('dp')
- grad_enc_qkv_weight: float32 [768, 2304], P('dp')
- grad_enc_query_bias: float32 [768], P('dp')
- grad_enc_value_bias: float32 [768], P('dp')
- grad_enc_out_weight: float32 [768, 768], P('dp')
- grad_enc_out_bias: float32 [768], P('dp')
- grad_enc_norm2_gain: float32 [768], P('dp')
- grad_enc_norm2_bias: float32 [768], P('dp')
- grad_enc_up_weight: float32 [768, 3072], P('dp')
- grad_enc_up_bias: float32 [3072], P('dp')
- grad_enc_down_weight: float32 [3072, 768], P('dp')
- grad_enc_down_bias: float32 [768], P('dp')
- grad_emb_weight: float32 [768, 512], P('dp')
- grad_emb_bias: float32 [512], P('dp')
- grad_mask_token: float32 [512], P('dp')
- grad_dec_norm1_gain: float32 [512], P('dp')
- grad_dec_norm1_bias: float32 [512], P('dp')
- grad_dec_qkv_weight: float32 [512, 1536], P('dp')
- grad_dec_query_bias: float32 [512], P('dp')
- grad_dec_value_bias: float32 [512], P('dp')
- grad_dec_out_weight: float32 [512, 512], P('dp')
- grad_dec_out_bias: float32 [512], P('dp')
- grad_dec_norm2_gain: float32 [512], P('dp')
- grad_dec_norm2_bias: float32 [512], P('dp')
- grad_dec_up_weight: float32 [512, 2048], P('dp')
- grad_dec_up_bias: float32 [2048], P('dp')
- grad_dec_down_weight: float32 [2048, 512], P('dp')
- grad_dec_down_bias: float32 [512], P('dp')
Inputs may be any that keep to these rules, and one draw needn't show every extreme that they name: `vis_slot`: in every strip, each aligned run of 512 entries lists distinct positions in increasing order within one block of 672 positions; the block's first and last positions are always listed. `seg_ids`: segment ids never fall along a strip; a segment spans 1 to 840 positions.
All inputs are finite; a program needn't handle non-finite values.
Results may differ from a plain program's by a relative error of at most 0.025.
Values may be sent and summed in bfloat16 or wider, within the bound.
A program may use at most 384 MiB of HBM per device.

v0:
```python
import jax
import jax.numpy as jnp
from jax import lax
from jax.sharding import PartitionSpec as P

HEADS_ENC = 12
HEADS_DEC = 16


EPSILON = 1e-06


def layer_norm(values, gain, bias):
    centre = jnp.mean(values, axis=-1, keepdims=True)
    centred = values - centre
    spread = jnp.mean(centred * centred, axis=-1, keepdims=True)
    return centred * lax.rsqrt(spread + EPSILON) * gain + bias


def split_heads(values, head_count):
    return values.reshape(
        values.shape[0], values.shape[1], head_count, values.shape[2] // head_count
    )


def forward_attention(queries, key_rows, value_rows, segments, head_count):
    strips_here, rows_here, model_width = queries.shape
    head_size = model_width // head_count
    scale = float(head_size) ** (-0.5)
    all_keys, all_values, all_segments = (
        lax.all_gather(key_rows, "blk", axis=1, tiled=True),
        lax.all_gather(value_rows, "blk", axis=1, tiled=True),
        lax.all_gather(segments, "blk", axis=1, tiled=True),
    )
    scores = (
        jnp.einsum(
            "srhd,skhd->srhk",
            split_heads(queries, head_count),
            split_heads(all_keys, head_count),
            preferred_element_type=jnp.float32,
        )
        * scale
    )
    allowed = segments[:, :, None, None] == all_segments[:, None, None, :]
    scores = jnp.where(allowed, scores, -1e30)
    peak = jnp.max(scores, axis=-1)
    raised = jnp.where(allowed, jnp.exp(scores - peak[..., None]), 0.0)
    total = jnp.sum(raised, axis=-1)
    probs = (raised / total[..., None]).astype(jnp.bfloat16)
    weighted = jnp.einsum(
        "srhk,skhd->srhd",
        probs,
        split_heads(all_values, head_count),
        preferred_element_type=jnp.float32,
    )
    attended = weighted.reshape(strips_here, rows_here, model_width)
    logsum = peak + jnp.log(total)
    return (attended, logsum, (all_keys, all_values, all_segments))


def gradient_terms(
    queries,
    out_grad,
    logsum,
    row_dots,
    query_segments,
    key_rows,
    value_rows,
    key_segments,
    head_count,
):
    strips_here, rows_here, model_width = queries.shape
    key_count = key_rows.shape[1]
    query_heads = split_heads(queries, head_count)
    grad_heads = split_heads(out_grad, head_count)
    key_heads = split_heads(key_rows, head_count)
    value_heads = split_heads(value_rows, head_count)
    scale = float(query_heads.shape[-1]) ** (-0.5)
    scores = (
        jnp.einsum("srhd,skhd->srhk", query_heads, key_heads, preferred_element_type=jnp.float32)
        * scale
    )
    allowed = query_segments[:, :, None, None] == key_segments[:, None, None, :]
    probs = jnp.where(allowed, jnp.exp(scores - logsum[..., None]), 0.0)
    prob_grads = jnp.einsum(
        "srhd,skhd->srhk", grad_heads, value_heads, preferred_element_type=jnp.float32
    )
    score_grads = (probs * (prob_grads - row_dots[..., None])).astype(jnp.bfloat16)
    d_query = (
        jnp.einsum("srhk,skhd->srhd", score_grads, key_heads, preferred_element_type=jnp.float32)
        * scale
    )
    d_key = (
        jnp.einsum("srhk,srhd->skhd", score_grads, query_heads, preferred_element_type=jnp.float32)
        * scale
    )
    d_value = jnp.einsum(
        "srhk,srhd->skhd",
        probs.astype(jnp.bfloat16),
        grad_heads,
        preferred_element_type=jnp.float32,
    )
    return (
        d_query.reshape(strips_here, rows_here, model_width),
        d_key.reshape(strips_here, key_count, model_width),
        d_value.reshape(strips_here, key_count, model_width),
    )


def backward_attention(queries, segments, gathered, out_grad, attended, logsum, head_count):
    row_dots = jnp.sum(
        split_heads(out_grad.astype(jnp.float32), head_count) * split_heads(attended, head_count),
        axis=-1,
    )
    all_keys, all_values, all_segments = gathered
    d_query, key_terms, value_terms = gradient_terms(
        queries,
        out_grad,
        logsum,
        row_dots,
        segments,
        all_keys,
        all_values,
        all_segments,
        head_count,
    )
    d_key, d_value = (
        lax.psum_scatter(
            key_terms.astype(jnp.bfloat16), "blk", scatter_dimension=1, tiled=True
        ).astype(jnp.float32),
        lax.psum_scatter(
            value_terms.astype(jnp.bfloat16), "blk", scatter_dimension=1, tiled=True
        ).astype(jnp.float32),
    )
    return (d_query, d_key, d_value)


def block_forward(residual, segments, weights, head_count):
    (
        norm1_gain,
        norm1_bias,
        qkv_weight,
        query_bias,
        value_bias,
        out_weight,
        out_bias,
        norm2_gain,
        norm2_bias,
        up_weight,
        up_bias,
        down_weight,
        down_bias,
    ) = weights
    model_width = residual.shape[-1]
    normed = layer_norm(
        residual, norm1_gain.astype(jnp.float32), norm1_bias.astype(jnp.float32)
    ).astype(jnp.bfloat16)
    projected = jnp.dot(normed, qkv_weight, preferred_element_type=jnp.float32)
    queries = (projected[..., :model_width] + query_bias.astype(jnp.float32)).astype(jnp.bfloat16)
    key_rows = projected[..., model_width : 2 * model_width].astype(jnp.bfloat16)
    value_rows = (projected[..., 2 * model_width :] + value_bias.astype(jnp.float32)).astype(
        jnp.bfloat16
    )
    attended, logsum, gathered = forward_attention(
        queries, key_rows, value_rows, segments, head_count
    )
    attended_low = attended.astype(jnp.bfloat16)
    middle = residual + (
        jnp.dot(attended_low, out_weight, preferred_element_type=jnp.float32)
        + out_bias.astype(jnp.float32)
    )
    normed_two = layer_norm(
        middle, norm2_gain.astype(jnp.float32), norm2_bias.astype(jnp.float32)
    ).astype(jnp.bfloat16)
    pre_act = jnp.dot(normed_two, up_weight, preferred_element_type=jnp.float32) + up_bias.astype(
        jnp.float32
    )
    hidden = jax.nn.gelu(pre_act, approximate=False).astype(jnp.bfloat16)
    result = middle + (
        jnp.dot(hidden, down_weight, preferred_element_type=jnp.float32)
        + down_bias.astype(jnp.float32)
    )
    kept = (
        residual,
        normed,
        queries,
        key_rows,
        value_rows,
        gathered,
        attended,
        logsum,
        attended_low,
        middle,
        normed_two,
        pre_act,
        hidden,
    )
    return (result, kept)


def block_backward(upstream, kept, weights, segments, head_count):
    (
        norm1_gain,
        norm1_bias,
        qkv_weight,
        query_bias,
        value_bias,
        out_weight,
        out_bias,
        norm2_gain,
        norm2_bias,
        up_weight,
        up_bias,
        down_weight,
        down_bias,
    ) = weights
    (
        residual,
        normed,
        queries,
        key_rows,
        value_rows,
        gathered,
        attended,
        logsum,
        attended_low,
        middle,
        normed_two,
        pre_act,
        hidden,
    ) = kept
    d_down = upstream.astype(jnp.bfloat16)
    grad_down_bias = jnp.sum(d_down.astype(jnp.float32), axis=(0, 1))
    grad_down = jnp.einsum("srf,srw->fw", hidden, d_down, preferred_element_type=jnp.float32)
    d_hidden = jnp.einsum("srw,fw->srf", d_down, down_weight, preferred_element_type=jnp.float32)
    unused_act, gelu_pull = jax.vjp(
        lambda inner_vals: jax.nn.gelu(inner_vals, approximate=False), pre_act
    )
    d_pre = gelu_pull(d_hidden)[0].astype(jnp.bfloat16)
    grad_up_bias = jnp.sum(d_pre.astype(jnp.float32), axis=(0, 1))
    grad_up = jnp.einsum("srw,srf->wf", normed_two, d_pre, preferred_element_type=jnp.float32)
    d_normed_two = jnp.einsum("srf,wf->srw", d_pre, up_weight, preferred_element_type=jnp.float32)
    unused_two, norm_two_pull = jax.vjp(
        layer_norm, middle, norm2_gain.astype(jnp.float32), norm2_bias.astype(jnp.float32)
    )
    d_middle, grad_norm2_gain, grad_norm2_bias = norm_two_pull(d_normed_two)
    d_middle = d_middle + upstream
    d_branch = d_middle.astype(jnp.bfloat16)
    grad_out_bias = jnp.sum(d_branch.astype(jnp.float32), axis=(0, 1))
    grad_out = jnp.einsum("srw,srv->wv", attended_low, d_branch, preferred_element_type=jnp.float32)
    d_attended = jnp.einsum(
        "srv,wv->srw", d_branch, out_weight, preferred_element_type=jnp.float32
    ).astype(jnp.bfloat16)
    d_query, d_key, d_value = backward_attention(
        queries, segments, gathered, d_attended, attended, logsum, head_count
    )
    d_query = d_query.astype(jnp.bfloat16)
    d_key = d_key.astype(jnp.bfloat16)
    d_value = d_value.astype(jnp.bfloat16)
    grad_query_bias = jnp.sum(d_query.astype(jnp.float32), axis=(0, 1))
    grad_value_bias = jnp.sum(d_value.astype(jnp.float32), axis=(0, 1))
    d_projected = jnp.concatenate([d_query, d_key, d_value], axis=-1)
    grad_qkv = jnp.einsum("srw,srx->wx", normed, d_projected, preferred_element_type=jnp.float32)
    d_normed = jnp.einsum(
        "srx,wx->srw", d_projected, qkv_weight, preferred_element_type=jnp.float32
    )
    unused_one, norm_one_pull = jax.vjp(
        layer_norm, residual, norm1_gain.astype(jnp.float32), norm1_bias.astype(jnp.float32)
    )
    d_residual, grad_norm1_gain, grad_norm1_bias = norm_one_pull(d_normed)
    d_residual = d_residual + d_middle
    gradients = (
        grad_norm1_gain,
        grad_norm1_bias,
        grad_qkv,
        grad_query_bias,
        grad_value_bias,
        grad_out,
        grad_out_bias,
        grad_norm2_gain,
        grad_norm2_bias,
        grad_up,
        grad_up_bias,
        grad_down,
        grad_down_bias,
    )
    return (d_residual, gradients)


def reduce_gradients(gradients):
    dp_count = lax.axis_size("dp")
    blk_count = lax.axis_size("blk")
    packed = jnp.concatenate([gradient.reshape(dp_count, -1) for gradient in gradients], axis=1)
    width_all = packed.shape[1]
    stacked = packed.reshape(dp_count * blk_count, width_all // blk_count)
    share = lax.psum_scatter(stacked, ("dp", "blk"), scatter_dimension=0, tiled=True)
    summed = (
        lax.all_gather(share.astype(jnp.bfloat16), "blk", axis=0, tiled=True)
        .astype(share.dtype)
        .reshape(1, width_all)
    )
    flattened = summed.reshape(-1)
    shares = []
    offset = 0
    for gradient in gradients:
        length = gradient.size // dp_count
        shape_here = (gradient.shape[0] // dp_count,) + gradient.shape[1:]
        shares.append(flattened[offset : offset + length].reshape(shape_here))
        offset = offset + length
    return tuple(shares)


def per_device(
    patches,
    vis_slot,
    seg_ids,
    enc_norm1_gain,
    enc_norm1_bias,
    enc_qkv_weight,
    enc_query_bias,
    enc_value_bias,
    enc_out_weight,
    enc_out_bias,
    enc_norm2_gain,
    enc_norm2_bias,
    enc_up_weight,
    enc_up_bias,
    enc_down_weight,
    enc_down_bias,
    emb_weight,
    emb_bias,
    mask_token,
    dec_norm1_gain,
    dec_norm1_bias,
    dec_qkv_weight,
    dec_query_bias,
    dec_value_bias,
    dec_out_weight,
    dec_out_bias,
    dec_norm2_gain,
    dec_norm2_bias,
    dec_up_weight,
    dec_up_bias,
    dec_down_weight,
    dec_down_bias,
    cotangent,
):
    enc_weights = (
        enc_norm1_gain,
        enc_norm1_bias,
        enc_qkv_weight,
        enc_query_bias,
        enc_value_bias,
        enc_out_weight,
        enc_out_bias,
        enc_norm2_gain,
        enc_norm2_bias,
        enc_up_weight,
        enc_up_bias,
        enc_down_weight,
        enc_down_bias,
    )
    dec_weights = (
        dec_norm1_gain,
        dec_norm1_bias,
        dec_qkv_weight,
        dec_query_bias,
        dec_value_bias,
        dec_out_weight,
        dec_out_bias,
        dec_norm2_gain,
        dec_norm2_bias,
        dec_up_weight,
        dec_up_bias,
        dec_down_weight,
        dec_down_bias,
    )
    vis_segments = jnp.take_along_axis(seg_ids, vis_slot, axis=1)
    encoded, enc_kept = block_forward(
        patches.astype(jnp.float32), vis_segments, enc_weights, HEADS_ENC
    )
    encoded_low = encoded.astype(jnp.bfloat16)
    span_rows = seg_ids.shape[1]
    onehot = (vis_slot[:, None, :] == lax.broadcasted_iota(jnp.int32, (1, span_rows, 1), 1)).astype(
        jnp.bfloat16
    )
    placed = jnp.einsum(
        "spv,sve->spe", onehot, encoded_low, preferred_element_type=jnp.float32
    ).astype(jnp.bfloat16)
    visible_rows = jnp.sum(onehot.astype(jnp.float32), axis=-1)[..., None]
    dec_in = (
        jnp.dot(placed, emb_weight, preferred_element_type=jnp.float32)
        + visible_rows * emb_bias.astype(jnp.float32)
        + (1.0 - visible_rows) * mask_token.astype(jnp.float32)
    )
    decoded, dec_kept = block_forward(dec_in, seg_ids, dec_weights, HEADS_DEC)
    d_dec_in, dec_grads = block_backward(
        cotangent.astype(jnp.float32), dec_kept, dec_weights, seg_ids, HEADS_DEC
    )
    grad_emb_bias = jnp.sum(d_dec_in * visible_rows, axis=(0, 1))
    grad_mask = jnp.sum(d_dec_in * (1.0 - visible_rows), axis=(0, 1))
    d_dec_low = d_dec_in.astype(jnp.bfloat16)
    grad_emb = jnp.einsum("spe,spc->ec", placed, d_dec_low, preferred_element_type=jnp.float32)
    d_placed = jnp.einsum("spc,ec->spe", d_dec_low, emb_weight, preferred_element_type=jnp.float32)
    d_encoded = jnp.take_along_axis(d_placed, vis_slot[..., None], axis=1)
    d_patches, enc_grads = block_backward(d_encoded, enc_kept, enc_weights, vis_segments, HEADS_ENC)
    gradients = enc_grads + (grad_emb, grad_emb_bias, grad_mask) + dec_grads
    shares = reduce_gradients(gradients)
    return (decoded.astype(jnp.bfloat16), d_patches.astype(jnp.bfloat16)) + shares


def solution(mesh):
    return jax.shard_map(
        per_device,
        mesh=mesh,
        in_specs=(
            P("dp", "blk", None),
            P("dp", "blk"),
            P("dp", "blk"),
            P(),
            P(),
            P(),
            P(),
            P(),
            P(),
            P(),
            P(),
            P(),
            P(),
            P(),
            P(),
            P(),
            P(),
            P(),
            P(),
            P(),
            P(),
            P(),
            P(),
            P(),
            P(),
            P(),
            P(),
            P(),
            P(),
            P(),
            P(),
            P(),
            P("dp", "blk", None),
        ),
        out_specs=(
            P("dp", "blk", None),
            P("dp", "blk", None),
            P("dp"),
            P("dp"),
            P("dp", None),
            P("dp"),
            P("dp"),
            P("dp", None),
            P("dp"),
            P("dp"),
            P("dp"),
            P("dp", None),
            P("dp"),
            P("dp", None),
            P("dp"),
            P("dp", None),
            P("dp"),
            P("dp"),
            P("dp"),
            P("dp"),
            P("dp", None),
            P("dp"),
            P("dp"),
            P("dp", None),
            P("dp"),
            P("dp"),
            P("dp"),
            P("dp", None),
            P("dp"),
            P("dp", None),
            P("dp"),
        ),
        check_vma=False,
    )
```

profile of v0, /device:TPU:0, one launch (start us, length us, event | category | flops | bytes accessed | tf_op | source)
XLA Modules:
  0.0 1599.0 jit_solution(14021032755284695979)
XLA Ops:
  50.9 14.4 fusion.21
  65.9 12.1 fusion.23
  80.5 13.4 bitcast_convert_fusion
  95.3 19.9 %multiply_convert_fusion = (bf16[512,3072]{1,0:T(8,128)(2,1)}, f32[512,3072]{1,0:T(8,128)}, f32[512,3072]{1,0:T(8,128)}) fusion(f32[3072]{0:T(1024)S(1)} %copy-done.67, bf16[768,3072]{1,0:T(8,128)(2,1)} %param.45, f32[1,512,768]{2,1,0:T(8,128)S(1)} %get-tuple-element.91, f32[768]{0:T(1024)S(1)} %copy-done.81, f32[768]{0:T(1024)S(1)} %convert_element_type.434, ...), kind=kOutput, calls=%fused_computation.46 | convolution fusion | flops 2521694208 | bytes 22042624 | tf_op jit(solution)/shard_map/dot_general | solution.py:175
  159.9 26.2 %fusion.4 = (f32[672,16]{0,1:T(8,128)}, f32[16,1344,672]{1,2,0:T(8,128)}) fusion(pred[672,1344]{1,0:T(8,128)(4,1)} %broadcast_compare_fusion, bf16[1344,16,32]{0,2,1:T(8,128)(2,1)} %bitcast.357, bf16[672,16,32]{0,2,1:T(8,128)(2,1)} %bitcast.374), kind=kOutput, calls=%fused_computation.11 | convolution fusion | flops 968185344 | bytes 60813312 | tf_op jit(solution)/shard_map/srhd,skhd->srhk/dot_general | solution.py:36
  186.1 30.3 %fusion.6 = f32[672,16]{0,1:T(8,128)} fusion(f32[16,1344,672]{1,2,0:T(8,128)} %get-tuple-element.96, f32[672,16]{0,1:T(8,128)} %get-tuple-element.95, pred[672,1344]{1,0:T(8,128)(4,1)} %broadcast_compare_fusion), kind=kLoop, calls=%fused_computation.13 | loop fusion | flops 72242688 | bytes 58791936 | tf_op jit(solution)/shard_map/reduce_sum | solution.py:48
  220.4 26.9 %bitcast_convert_fusion.1 = (bf16[1,672,16,32]{1,3,2,0:T(8,128)(2,1)}, f32[16,32,672]{2,1,0:T(8,128)}) fusion(bf16[1344,16,32]{0,2,1:T(8,128)(2,1)} %bitcast.389, f32[672,16]{0,1:T(8,128)} %fusion.6, f32[672,16]{0,1:T(8,128)} %get-tuple-element.95, f32[16,1344,672]{1,2,0:T(8,128)} %get-tuple-element.96, pred[672,1344]{1,0:T(8,128)(4,1)} %broadcast_compare_fusion), kind=kOutput, calls=%fused_computation.121 | convolution fusion | flops 1011892224 | bytes 62232576 | tf_op jit(solution)/shard_map/srhk,skhd->srhd/dot_general | solution.py:50
  250.3 14.4 multiply_convert_fusion.1
  284.0 38.7 %fusion.1 = bf16[1,672,16,1344]{3,1,2,0:T(8,128)(2,1)} fusion(f32[16,1344,672]{1,2,0:T(8,128)} %get-tuple-element.96, bf16[1344,16,32]{0,2,1:T(8,128)(2,1)} %bitcast.390, bf16[672,16,32]{0,2,1:T(8,128)(2,1)} %bitcast.400, f32[672,16]{0,1:T(8,128)} %fusion.71, f32[672,16]{0,1:T(8,128)} %log_add_fusion, pred[672,1344]{1,0:T(8,128)(4,1)} %broadcast_compare_fusion), kind=kOutput, calls=%fused_computation.4 | convolution fusion | flops 1011548160 | bytes 89757696 | tf_op jit(solution)/shard_map/srhd,skhd->srhk/dot_general | solution.py:85
  322.7 15.7 fusion.46
  349.8 23.9 %fusion.49 = bf16[16,32,1344]{2,1,0:T(8,128)(2,1)} fusion(bf16[672,16,32]{0,2,1:T(8,128)(2,1)} %bitcast.401, f32[16,1344,672]{1,2,0:T(8,128)} %get-tuple-element.96, f32[672,16]{0,1:T(8,128)} %log_add_fusion, pred[672,1344]{1,0:T(8,128)(4,1)} %broadcast_compare_fusion), kind=kOutput, calls=%fused_computation.82 | convolution fusion | flops 983334912 | bytes 60813312 | tf_op jit(solution)/shard_map/srhk,srhd->skhd/dot_general | solution.py:97
  387.2 16.9 %convert_reduce_fusion.5 = (f32[16,32]{1,0:T(8,128)}, bf16[16,32,672]{2,1,0:T(8,128)(2,1)}) fusion(bf16[1344,16,32]{0,2,1:T(8,128)(2,1)} %bitcast.358, bf16[1,672,16,1344]{3,1,2,0:T(8,128)(2,1)} %fusion.1), kind=kOutput, calls=%fused_computation.126 | convolution fusion | flops 926219776 | bytes 30967808 | tf_op jit(solution)/shard_map/srhk,skhd->srhd/dot_general | solution.py:90
  433.0 11.5 convert_reduce_fusion
  465.2 16.0 %fusion.25 = bf16[512,12,1024]{0,2,1:T(8,128)(2,1)} fusion(f32[12,1024,512]{2,1,0:T(8,128)} %get-tuple-element.87, f32[512,12]{0,1:T(8,128)} %fusion.69, f32[512,12]{0,1:T(8,128)} %log_add_fusion.1, pred[512,1024]{0,1:T(8,128)(4,1)} %broadcast_compare_fusion.1, bf16[1024,12,64]{0,2,1:T(8,128)(2,1)} %bitcast.387, bf16[512,12,64]{0,2,1:T(8,128)(2,1)} %bitcast.398), kind=kOutput, calls=%fused_computation.36 | convolution fusion | flops 843055104 | bytes 40681472 | tf_op jit(solution)/shard_map/srhd,skhd->srhk/dot_general | solution.py:85
  520.6 12.3 fusion.58
  651.5 20.5 %dynamic-update-slice.3 = f32[16,664576]{1,0:T(8,128)} dynamic-update-slice(f32[16,664576]{1,0:T(8,128)} %dynamic-update-slice.2, f32[16,110592]{1,0:T(8,128)} %reshape.1410, s32[]{} %constant.92, s32[]{} %constant.94) | dynamic-update-slice | bytes 14155780
  687.4 27.4 %dynamic-update-slice.10 = f32[16,664576]{1,0:T(8,128)} dynamic-update-slice(f32[16,664576]{1,0:T(8,128)} %dynamic-update-slice.9, f32[16,147456]{1,0:T(8,128)} %reshape.1417, s32[]{} %constant.92, s32[]{} %constant.185) | dynamic-update-slice | bytes 18874372
  716.3 27.4 %dynamic-update-slice.12 = f32[16,664576]{1,0:T(8,128)} dynamic-update-slice(f32[16,664576]{1,0:T(8,128)} %dynamic-update-slice.11, f32[16,147456]{1,0:T(8,128)} %reshape.1419, s32[]{} %constant.92, s32[]{} %constant.187) | dynamic-update-slice | bytes 18874372
  757.6 10.8 dynamic-update-slice.19
  777.9 13.6 dynamic-update-slice.26
  792.9 13.1 dynamic-update-slice.28
  807.4 34.8 %reshape.1436 = f32[32,332288]{1,0:T(8,128)} reshape(f32[16,664576]{1,0:T(8,128)} %dynamic-update-slice.29) | data formatting | bytes 85065728 | tf_op jit(solution)/shard_map/reshape | solution.py:295
  842.1 678.7 %all-reduce.3 = bf16[32,332288]{1,0:T(8,128)(2,1)} all-reduce(f32[32,332288]{1,0:T(8,128)} %reshape.1436), channel_id=6, replica_groups=mesh['dp'=16,'blk'=2] {'dp','blk'}, use_global_device_ids=true, to_apply=%region_47.48.clone | all-reduce | flops 10633216 | bytes 63799296
  1532.9 30.4 %all-gather.15.cloned.1.call-done = bf16[2,1,332288]{2,1,0:T(2,128)(2,1)} async-done(((bf16[1,1,332288]{2,1,0:T(2,128)(2,1)}), bf16[2,1,332288]{2,1,0:T(2,128)(2,1)}) %all-gather.15.cloned.1.call-update) | async-done | bytes 1329168 | tf_op jit(solution)/shard_map/all_gather | solution.py:298
  (410 shorter events, 433.9 us)
Async XLA Ops:
  7.2 41.0 %all-gather.9.cloned.1.call-start = ((), (), s32[]{:S(2)}) async-start(), calls=%async_computation.5 | async-start | bytes 2359296 | tf_op jit(solution)/shard_map/all_gather | solution.py:31
  18.1 59.8 %all-gather.7.cloned.1.call-start = ((), (), s32[]{:S(2)}) async-start(), calls=%async_computation.4 | async-start | bytes 2359296 | tf_op jit(solution)/shard_map/all_gather | solution.py:32
  21.6 135.3 %all-gather.13.cloned.1.call-start = ((), (), s32[]{:S(2)}) async-start(), calls=%async_computation.7 | async-start | bytes 2064384 | tf_op jit(solution)/shard_map/all_gather | solution.py:31
  33.8 61.5 %copy-start.62 = (f32[768]{0:T(1024)}, f32[768]{0:T(1024)S(1)}, u32[]{:S(2)}) copy-start(f32[768]{0:T(1024)S(1)} %convert_element_type.434) | copy-start | bytes 9220
  37.9 85.6 %copy-start.40 = (f32[672]{0:T(1024)}, f32[672]{0:T(1024)S(1)}, u32[]{:S(2)}) copy-start(f32[672]{0:T(1024)S(1)} %convert_reduce_fusion.11) | copy-start | bytes 8068
  50.9 15.0 copy-start.15
  80.5 13.5 copy-start.91
  94.9 20.3 %copy-start.12 = (f32[1,512,768]{2,1,0:T(8,128)}, f32[1,512,768]{2,1,0:T(8,128)S(1)}, u32[]{:S(2)}) copy-start(f32[1,512,768]{2,1,0:T(8,128)S(1)} %get-tuple-element.91) | copy-start | bytes 4718596
  95.0 20.3 %copy-start.51 = (f32[512]{0:T(512)}, f32[512]{0:T(512)S(1)}, u32[]{:S(2)}) copy-start(f32[512]{0:T(512)S(1)} %broadcast_multiply_fusion.2) | copy-start | bytes 6148
  95.3 19.9 %copy-start.56 = (f32[512]{0:T(512)}, f32[512]{0:T(512)S(1)}, u32[]{:S(2)}) copy-start(f32[512]{0:T(512)S(1)} %multiply_reduce_fusion) | copy-start | bytes 6148
  95.3 19.9 %copy-start.71 = (f32[512]{0:T(512)}, f32[512]{0:T(512)S(1)}, u32[]{:S(2)}) copy-start(f32[512]{0:T(512)S(1)} %fusion.114) | copy-start | bytes 6148
  131.3 86.6 %all-gather.11.cloned.1.call-start = ((), (), s32[]{:S(2)}) async-start(), calls=%async_computation.6 | async-start | bytes 2064384 | tf_op jit(solution)/shard_map/all_gather | solution.py:32
  153.4 250.8 %reduce-scatter.13.cloned.1.call-start = ((), (), s32[]{:S(2)}) async-start(), calls=%async_computation.11 | async-start | bytes 2064384
  220.4 27.0 %copy-start.74 = (f32[512]{0:T(512)S(1)}, f32[512]{0:T(512)}, u32[]{:S(2)}) copy-start(f32[512]{0:T(512)} %convert_element_type.456) | copy-start | bytes 6148
  249.9 21.7 %copy-start.1 = (f32[672,512]{1,0:T(8,128)}, f32[672,512]{1,0:T(8,128)S(1)}, u32[]{:S(2)}) copy-start(f32[672,512]{1,0:T(8,128)S(1)} %get-tuple-element.100) | copy-start | bytes 4128772
  250.3 14.4 copy-start.21
  250.3 14.4 copy-start.89
  349.4 61.4 %reduce-scatter.15.cloned.1.call-start = ((), (), s32[]{:S(2)}) async-start(), calls=%async_computation.12 | async-start | bytes 2064384
  384.6 234.7 %reduce-scatter.9.cloned.1.call-start = ((), (), s32[]{:S(2)}) async-start(), calls=%async_computation.8 | async-start | bytes 2359296 | tf_op jit(solution)/shard_map/reduce_scatter | solution.py:128
  491.1 128.2 %reduce-scatter.11.cloned.1.call-start = ((), (), s32[]{:S(2)}) async-start(), calls=%async_computation.9 | async-start | bytes 2359296 | tf_op jit(solution)/shard_map/reduce_scatter | solution.py:131
  532.9 1030.4 %all-gather.15.cloned.1.call-start = ((), (), s32[]{:S(2)}) async-start(), calls=%async_computation.10 | async-start | bytes 3987456 | tf_op jit(solution)/shard_map/all_gather | solution.py:298
  757.6 17.4 %copy-start.45 = (f32[16,32]{1,0:T(8,128)S(1)}, f32[16,32]{1,0:T(8,128)}, u32[]{:S(2)}) copy-start(f32[16,32]{1,0:T(8,128)} %reshape.1430) | copy-start | bytes 6148
  757.6 18.9 %copy-start.44 = (f32[16,32]{1,0:T(8,128)S(1)}, f32[16,32]{1,0:T(8,128)}, u32[]{:S(2)}) copy-start(f32[16,32]{1,0:T(8,128)} %reshape.1431) | copy-start | bytes 6148
  777.9 13.6 copy-start.75
  (79 other events, 387.4 us)
Sparse Core Ops, SparseCore 0:
  18.2 29.9 all-gather.8
  49.8 27.1 all-gather.6
  131.4 25.4 all-gather.12
  158.3 24.9 all-gather.10
  349.5 24.1 reduce-scatter.12
  384.8 24.1 reduce-scatter.14
  491.2 26.1 reduce-scatter.8
  533.0 26.1 reduce-scatter.10
  1526.0 37.2 all-gather.14
where the time goes:
time: 1610 us; the launch traced here: 1600 us
  blocking collectives  689 us (43%)
  local copies, waits for them, and re-layouts  375 us (23%)
  matrix products  374 us (23%)
  other arithmetic  107 us (7%)
  waiting for transfers between devices  37.7 us (2%)
    unnamed x2, blocking collectives  683 us
    unnamed x228, local copies, waits for them, and re-layouts  212 us
    reshape x27, local copies, waits for them, and re-layouts, reduce_gradients(): gradient.reshape(dp_count, -1)  68.6 us
    dot_general x2, matrix products, gradient_terms(): jnp.einsum('srhd,skhd->srhk', grad_heads, value_heads, preferred_element_...  54.7 us
    reduce_sum x2, other arithmetic, forward_attention(): total = jnp.sum(raised, axis=-1)  42.4 us
    dot_general x2, matrix products, forward_attention(): jnp.einsum('srhd,skhd->srhk', split_heads(queries, head_count), split_hea...  40.6 us
    dot_general x2, matrix products, forward_attention(): jnp.einsum('srhk,skhd->srhd', probs, split_heads(all_values, head_count),...  40.4 us
    dot_general x2, matrix products, gradient_terms(): jnp.einsum('srhk,srhd->skhd', probs.astype(jnp.bfloat16), grad_heads, pre...  36.2 us
  transfers between devices with their start and end apart: 9, of which 3 were waited for; matrix products, arithmetic and copies ran while one was open for 20% of the time, Pallas kernels for 0%

commit v1 on v0

--- a/solution.py
+++ b/solution.py
@@ -1,10 +1,318 @@
+import functools
 import jax
 import jax.numpy as jnp
 from jax import lax
+from jax.experimental import pallas as pl
+from jax.experimental.pallas import tpu as pltpu
 from jax.sharding import PartitionSpec as P
 
 HEADS_ENC = 12
 HEADS_DEC = 16
+
+LN2 = 0.6931471805599453
+BIG = -(2.0 ** 100)
+NT = (((1,), (1,)), ((), ()))
+BQ = 256
+BK = 256
+
+
+def padded_rows(rows):
+    return -(-rows // 128) * 128 + 128
+
+
+def key_ranges(segments, rows):
+    blocks = -(-rows // BQ)
+    filled = jnp.concatenate([segments, jnp.full((blocks * BQ - rows,), 7, jnp.int32)])
+    filled = jnp.minimum(filled, segments[rows - 1]).reshape(blocks, BQ)
+    low = jnp.sum(segments[None, :] < filled[:, 0:1], axis=1)
+    high = jnp.sum(segments[None, :] <= filled[:, BQ - 1 :], axis=1)
+    start = low // 128
+    count = (high - start * 128 + BK - 1) // BK
+    return jnp.concatenate([start, count]).astype(jnp.int32)
+
+
+def lanes(rows, width=128):
+    return lax.broadcasted_iota(jnp.int32, (rows, width), 1)
+
+
+def attention_forward_kernel(
+    rows, head_size, ranges, q_ref, k_ref, v_ref, seg_ref, out_ref, lse_ref, ka, va, qa, sc, acc
+):
+    heads = 128 // head_size
+    group = pl.program_id(0)
+    block = pl.program_id(1)
+    blocks = pl.num_programs(1)
+    padded = ka.shape[0]
+
+    @pl.when(block == 0)
+    def _():
+        marks = jnp.where(lanes(rows) == seg_ref[0:rows, :], 0.0, BIG)
+        marks = jnp.where(lanes(rows) < 8, marks, 0.0)
+        ka[0:rows, 0:128] = k_ref[...]
+        ka[0:rows, 128:256] = marks.astype(jnp.bfloat16)
+        va[0:rows, 0:128] = v_ref[...]
+        va[0:rows, 128:256] = jnp.ones((rows, 128), jnp.bfloat16)
+        rest = padded - rows
+        ka[rows:padded, 0:128] = jnp.zeros((rest, 128), jnp.bfloat16)
+        ka[rows:padded, 128:256] = jnp.where(lanes(rest) < 8, BIG, 0.0).astype(jnp.bfloat16)
+        va[rows:padded, :] = jnp.zeros((rest, 256), jnp.bfloat16)
+
+    first = pl.multiple_of(block * BQ, BQ)
+    lane = lanes(BQ)
+    marks = jnp.where(lane == seg_ref[pl.ds(first, BQ), :], 1.0, 0.0).astype(jnp.bfloat16)
+    queries = q_ref[...]
+    for head in range(heads):
+        here = lane // head_size == head
+        qa[head * BQ : (head + 1) * BQ, 0:128] = jnp.where(here, queries, jnp.zeros_like(queries))
+        qa[head * BQ : (head + 1) * BQ, 128:256] = marks
+
+    start = ranges[block] * 128
+    count = ranges[blocks + block]
+
+    def score(step, peak):
+        at = pl.multiple_of(start + step * BK, 128)
+        s = lax.dot_general(qa[...], ka[pl.ds(at, BK), :], NT, preferred_element_type=jnp.float32)
+        sc[step] = s
+        return jnp.maximum(peak, jnp.maximum(s[:, 0:128], s[:, 128:256]))
+
+    peak = lax.fori_loop(0, count, score, jnp.full((heads * BQ, 128), BIG, jnp.float32))
+    top = jnp.max(peak, axis=1, keepdims=True)
+    acc[...] = jnp.zeros_like(acc)
+
+    def weigh(step, carry):
+        at = pl.multiple_of(start + step * BK, 128)
+        p = jnp.exp2(sc[step] - top).astype(jnp.bfloat16)
+        acc[...] += jnp.dot(p, va[pl.ds(at, BK), :], preferred_element_type=jnp.float32)
+        return carry
+
+    lax.fori_loop(0, count, weigh, 0)
+    out = jnp.zeros((BQ, 128), jnp.float32)
+    lse = jnp.zeros((BQ, 128), jnp.float32)
+    for head in range(heads):
+        part = acc[head * BQ : (head + 1) * BQ, :]
+        total = part[:, 128:256]
+        out = jnp.where(lane // head_size == head, part[:, 0:128] / total, out)
+        lse = jnp.where(lane == 16 + head, top[head * BQ : (head + 1) * BQ] + jnp.log2(total), lse)
+    out_ref[...] = out.astype(jnp.bfloat16)
+    lse_ref[...] = lse
+
+
+def attention_forward(qkv, segments, ranges, head_size):
+    rows, width = qkv.shape
+    groups = width // 384
+    blocks = -(-rows // BQ)
+    padded = padded_rows(rows)
+    heads = 128 // head_size
+    steps = -(-padded // BK)
+    seg_column = jnp.concatenate(
+        [segments, jnp.full((blocks * BQ - rows,), 7, jnp.int32)]
+    ).reshape(-1, 1)
+    return pl.pallas_call(
+        functools.partial(attention_forward_kernel, rows, head_size),
+        grid_spec=pltpu.PrefetchScalarGridSpec(
+            num_scalar_prefetch=1,
+            grid=(groups, blocks),
+            in_specs=[
+                pl.BlockSpec((BQ, 128), lambda g, i, r: (i, g)),
+                pl.BlockSpec((rows, 128), lambda g, i, r: (0, groups + g)),
+                pl.BlockSpec((rows, 128), lambda g, i, r: (0, 2 * groups + g)),
+                pl.BlockSpec((blocks * BQ, 1), lambda g, i, r: (0, 0)),
+            ],
+            out_specs=[
+                pl.BlockSpec((BQ, 128), lambda g, i, r: (i, g)),
+                pl.BlockSpec((BQ, 128), lambda g, i, r: (i, g)),
+            ],
+            scratch_shapes=[
+                pltpu.VMEM((padded, 256), jnp.bfloat16),
+                pltpu.VMEM((padded, 256), jnp.bfloat16),
+                pltpu.VMEM((heads * BQ, 256), jnp.bfloat16),
+                pltpu.VMEM((steps, heads * BQ, BK), jnp.float32),
+                pltpu.VMEM((heads * BQ, 256), jnp.float32),
+            ],
+        ),
+        out_shape=[
+            jax.ShapeDtypeStruct((rows, groups * 128), jnp.bfloat16),
+            jax.ShapeDtypeStruct((rows, groups * 128), jnp.float32),
+        ],
+        name="attention_forward",
+    )(ranges, qkv, qkv, qkv, seg_column)
+
+
+def spread(values):
+    high = values.astype(jnp.bfloat16).astype(jnp.float32)
+    middle = (values - high).astype(jnp.bfloat16).astype(jnp.float32)
+    low = values - high - middle
+    return high + pltpu.roll(middle, 16, 1) + pltpu.roll(low, 32, 1)
+
+
+def attention_backward_kernel(
+    rows, head_size, ranges, q_ref, k_ref, v_ref, o_ref, do_ref, lse_ref, seg_ref,
+    dqkv_ref, bias_ref, ka, va, qa, da, qt, dt, dkt, dvt, dq
+):
+    heads = 128 // head_size
+    group = pl.program_id(0)
+    groups = pl.num_programs(0)
+    block = pl.program_id(1)
+    blocks = pl.num_programs(1)
+    padded = ka.shape[0]
+    scale = float(head_size) ** -0.5
+
+    @pl.when(block == 0)
+    def _():
+        lane = lanes(rows)
+        marks = jnp.where(lane == seg_ref[0:rows, :], 0.0, BIG)
+        ones = jnp.where((lane >= 16) & (lane < 64), 1.0, 0.0)
+        ka[0:rows, 0:128] = k_ref[...]
+        ka[0:rows, 128:256] = jnp.where(lane < 8, marks, ones).astype(jnp.bfloat16)
+        va[0:rows, 0:128] = v_ref[...]
+        va[0:rows, 128:256] = ones.astype(jnp.bfloat16)
+        rest = padded - rows
+        ka[rows:padded, 0:128] = jnp.zeros((rest, 128), jnp.bfloat16)
+        ka[rows:padded, 128:256] = jnp.where(lanes(rest) < 8, BIG, 0.0).astype(jnp.bfloat16)
+        va[rows:padded, :] = jnp.zeros((rest, 256), jnp.bfloat16)
+        dkt[...] = jnp.zeros_like(dkt)
+        dvt[...] = jnp.zeros_like(dvt)
+
+    first = pl.multiple_of(block * BQ, BQ)
+    lane = lanes(BQ)
+    left = rows - first
+    inside = lax.broadcasted_iota(jnp.int32, (BQ, 128), 0) < left
+    marks = jnp.where(lane == seg_ref[pl.ds(first, BQ), :], 1.0, 0.0)
+    queries = jnp.where(inside, q_ref[...].astype(jnp.float32), 0.0)
+    grads = jnp.where(inside, do_ref[...].astype(jnp.float32), 0.0)
+    product = jnp.where(inside, grads * o_ref[...].astype(jnp.float32), 0.0)
+    picks = (
+        lax.broadcasted_iota(jnp.int32, (128, 128), 0) // head_size + 16
+        == lax.broadcasted_iota(jnp.int32, (128, 128), 1)
+    )
+    picks = jnp.where(picks, 1.0, 0.0).astype(jnp.bfloat16)
+    product_high = product.astype(jnp.bfloat16)
+    product_low = (product - product_high.astype(jnp.float32)).astype(jnp.bfloat16)
+    dots = jnp.dot(product_high, picks, preferred_element_type=jnp.float32) + jnp.dot(
+        product_low, picks, preferred_element_type=jnp.float32
+    )
+    lse = jnp.where(inside, lse_ref[...], 0.0)
+    lse_terms = spread(-lse)
+    dot_terms = spread(-dots)
+    qt[...] = queries.T.astype(jnp.bfloat16)
+    dt[...] = grads.T.astype(jnp.bfloat16)
+    for head in range(heads):
+        here = lane // head_size == head
+        own = (lane == 16 + head) | (lane == 32 + head) | (lane == 48 + head)
+        at = slice(head * BQ, (head + 1) * BQ)
+        qa[at, 0:128] = jnp.where(here, queries, 0.0).astype(jnp.bfloat16)
+        qa[at, 128:256] = jnp.where(own, lse_terms, marks).astype(jnp.bfloat16)
+        da[at, 0:128] = jnp.where(here, grads, 0.0).astype(jnp.bfloat16)
+        da[at, 128:256] = jnp.where(own, dot_terms, 0.0).astype(jnp.bfloat16)
+    dq[...] = jnp.zeros_like(dq)
+    start = ranges[block] * 128
+    count = ranges[blocks + block]
+
+    def body(step, carry):
+        at = pl.multiple_of(start + step * BK, 128)
+        keys = ka[pl.ds(at, BK), :]
+        values = va[pl.ds(at, BK), :]
+        s = lax.dot_general(qa[...], keys, NT, preferred_element_type=jnp.float32)
+        p = jnp.exp2(s)
+        dp = lax.dot_general(da[...], values, NT, preferred_element_type=jnp.float32)
+        ds = (p * dp).astype(jnp.bfloat16)
+        p = p.astype(jnp.bfloat16)
+        dq[...] += jnp.dot(ds, keys[:, 0:128], preferred_element_type=jnp.float32)
+        for head in range(heads):
+            rows_in = slice(head * BQ, (head + 1) * BQ)
+            top = slice(head * head_size, (head + 1) * head_size)
+            dvt[top, pl.ds(at, BK)] += jnp.dot(
+                dt[top, :], p[rows_in], preferred_element_type=jnp.float32
+            )
+            dkt[top, pl.ds(at, BK)] += jnp.dot(
+                qt[top, :], ds[rows_in], preferred_element_type=jnp.float32
+            )
+        return carry
+
+    lax.fori_loop(0, count, body, 0)
+    out = jnp.zeros((BQ, 128), jnp.float32)
+    for head in range(heads):
+        out = jnp.where(lane // head_size == head, dq[head * BQ : (head + 1) * BQ, :], out)
+    out = jnp.where(inside, out * scale, 0.0)
+    column = pl.multiple_of(group * 128, 128)
+
+    @pl.when(block == 0)
+    def _():
+        bias_ref[:, pl.ds(column, 128)] = jnp.zeros((8, 128), jnp.float32)
+
+    bias_ref[0:1, pl.ds(column, 128)] += jnp.sum(out, axis=0, keepdims=True)
+    tail = rows - (rows // BQ) * BQ
+
+    if tail == 0:
+        dqkv_ref[pl.ds(first, BQ), pl.ds(column, 128)] = out.astype(jnp.bfloat16)
+    else:
+        @pl.when(block < blocks - 1)
+        def _():
+            dqkv_ref[pl.ds(first, BQ), pl.ds(column, 128)] = out.astype(jnp.bfloat16)
+
+        @pl.when(block == blocks - 1)
+        def _():
+            dqkv_ref[rows - tail : rows, pl.ds(column, 128)] = out[0:tail].astype(jnp.bfloat16)
+
+    @pl.when(block == blocks - 1)
+    def _():
+        k_column = pl.multiple_of((groups + group) * 128, 128)
+        v_column = pl.multiple_of((2 * groups + group) * 128, 128)
+        d_key = (dkt[...].T * LN2)[0:rows]
+        d_value = dvt[...].T[0:rows]
+        dqkv_ref[:, pl.ds(k_column, 128)] = d_key.astype(jnp.bfloat16)
+        dqkv_ref[:, pl.ds(v_column, 128)] = d_value.astype(jnp.bfloat16)
+        bias_ref[:, pl.ds(k_column, 128)] = jnp.zeros((8, 128), jnp.float32)
+        bias_ref[:, pl.ds(v_column, 128)] = jnp.broadcast_to(
+            jnp.sum(d_value, axis=0, keepdims=True), (8, 128)
+        )
+
+
+def attention_backward(qkv, attended, d_attended, lse, segments, ranges, head_size):
+    rows, width = qkv.shape
+    groups = width // 384
+    blocks = -(-rows // BQ)
+    padded = padded_rows(rows)
+    heads = 128 // head_size
+    seg_column = jnp.concatenate(
+        [segments, jnp.full((blocks * BQ - rows,), 7, jnp.int32)]
+    ).reshape(-1, 1)
+    return pl.pallas_call(
+        functools.partial(attention_backward_kernel, rows, head_size),
+        grid_spec=pltpu.PrefetchScalarGridSpec(
+            num_scalar_prefetch=1,
+            grid=(groups, blocks),
+            in_specs=[
+                pl.BlockSpec((BQ, 128), lambda g, i, r: (i, g)),
+                pl.BlockSpec((rows, 128), lambda g, i, r: (0, groups + g)),
+                pl.BlockSpec((rows, 128), lambda g, i, r: (0, 2 * groups + g)),
+                pl.BlockSpec((BQ, 128), lambda g, i, r: (i, g)),
+                pl.BlockSpec((BQ, 128), lambda g, i, r: (i, g)),
+                pl.BlockSpec((BQ, 128), lambda g, i, r: (i, g)),
+                pl.BlockSpec((blocks * BQ, 1), lambda g, i, r: (0, 0)),
+            ],
+            out_specs=[
+                pl.BlockSpec((rows, width), lambda g, i, r: (0, 0)),
+                pl.BlockSpec((8, width), lambda g, i, r: (0, 0)),
+            ],
+            scratch_shapes=[
+                pltpu.VMEM((padded, 256), jnp.bfloat16),
+                pltpu.VMEM((padded, 256), jnp.bfloat16),
+                pltpu.VMEM((heads * BQ, 256), jnp.bfloat16),
+                pltpu.VMEM((heads * BQ, 256), jnp.bfloat16),
+                pltpu.VMEM((128, BQ), jnp.bfloat16),
+                pltpu.VMEM((128, BQ), jnp.bfloat16),
+                pltpu.VMEM((128, padded), jnp.float32),
+                pltpu.VMEM((128, padded), jnp.float32),
+                pltpu.VMEM((heads * BQ, 128), jnp.float32),
+            ],
+        ),
+        out_shape=[
+            jax.ShapeDtypeStruct((rows, width), jnp.bfloat16),
+            jax.ShapeDtypeStruct((8, width), jnp.float32),
+        ],
+        name="attention_backward",
+    )(ranges, qkv, qkv, qkv, attended, d_attended, lse, seg_column)
 
 
 EPSILON = 1e-06
@@ -409,9 +717,257 @@
     return (decoded.astype(jnp.bfloat16), d_patches.astype(jnp.bfloat16)) + shares
 
 
+def pairs(count):
+    return [(i, i ^ 1) for i in range(count)]
+
+
+def to_partner(values):
+    return lax.ppermute(values, "dp", pairs(lax.axis_size("dp")))
+
+
+def relocate(values):
+    moves = []
+    for d in range(lax.axis_size("dp")):
+        for y in range(2):
+            moves.append((d * 2 + y, ((d & ~1) | y) * 2 + (d & 1)))
+    return lax.ppermute(values, ("dp", "blk"), moves)
+
+
+def join(mine, other, core, axis):
+    return jnp.where(
+        core == 0,
+        jnp.concatenate([mine, other], axis=axis),
+        jnp.concatenate([other, mine], axis=axis),
+    )
+
+
+def half(values, which, axis):
+    size = values.shape[axis] // 2
+    return lax.dynamic_slice_in_dim(values, which * size, size, axis)
+
+
+def own_heads(weight, core, parts):
+    width = weight.shape[-1] // (2 * parts)
+    split = weight.reshape(weight.shape[:-1] + (parts, 2, width))
+    picked = lax.dynamic_index_in_dim(split, core, axis=split.ndim - 2, keepdims=False)
+    return picked.reshape(weight.shape[:-1] + (parts * width,))
+
+
+def norm_parts(values):
+    centred = values - jnp.mean(values, axis=-1, keepdims=True)
+    spread = jnp.mean(centred * centred, axis=-1, keepdims=True)
+    return centred * lax.rsqrt(spread + EPSILON), lax.rsqrt(spread + EPSILON)
+
+
+def norm_backward(values, gain, upstream):
+    normal, inverse = norm_parts(values)
+    weighted = upstream * gain
+    lean = jnp.mean(weighted, axis=-1, keepdims=True)
+    along = jnp.mean(weighted * normal, axis=-1, keepdims=True)
+    return (
+        inverse * (weighted - lean - normal * along),
+        jnp.sum(upstream * normal, axis=0),
+        jnp.sum(upstream, axis=0),
+    )
+
+
+def wide(values):
+    return values.astype(jnp.float32)
+
+
+def low(values):
+    return values.astype(jnp.bfloat16)
+
+
+def times(left, right):
+    return jnp.dot(left, right, preferred_element_type=jnp.float32)
+
+
+def times_t(left, right):
+    return lax.dot_general(left, right, NT, preferred_element_type=jnp.float32)
+
+
+def t_times(left, right):
+    return lax.dot_general(left, right, (((0,), (0,)), ((), ())), preferred_element_type=jnp.float32)
+
+
+def strip_forward(residual, segments, ranges, weights, head_count, core):
+    (g1, b1, qkv_weight, q_bias, v_bias, out_w, out_b, g2, b2, up_w, up_b, down_w, down_b) = weights
+    width = residual.shape[-1]
+    head_size = width // head_count
+    own = width // 2
+    normed = low(layer_norm(residual, wide(g1), wide(b1)))
+    qkv_own = own_heads(qkv_weight, core, 3)
+    bias_own = jnp.concatenate(
+        [half(wide(q_bias), core, 0), jnp.zeros((own,), jnp.float32), half(wide(v_bias), core, 0)]
+    )
+    factor = jnp.where(jnp.arange(3 * own) < own, float(head_size) ** -0.5 / LN2, 1.0)
+    normed_all = join(normed, to_partner(normed), core, 0)
+    qkv = low((times(normed_all, qkv_own) + bias_own) * factor)
+    attended_own, logsum = attention_forward(qkv, segments, ranges, head_size)
+    received = to_partner(half(attended_own, 1 - core, 0))
+    attended = join(half(attended_own, core, 0), received, core, 1)
+    middle = residual + (times(attended, out_w) + wide(out_b))
+    normed_two = low(layer_norm(middle, wide(g2), wide(b2)))
+    pre_act = times(normed_two, up_w) + wide(up_b)
+    hidden = low(jax.nn.gelu(pre_act, approximate=False))
+    result = middle + (times(hidden, down_w) + wide(down_b))
+    kept = (
+        residual, normed_all, qkv_own, qkv, attended_own, logsum, attended, middle,
+        normed_two, pre_act, hidden,
+    )
+    return result, kept
+
+
+def strip_backward(upstream, kept, weights, segments, ranges, head_count, core):
+    (g1, b1, qkv_weight, q_bias, v_bias, out_w, out_b, g2, b2, up_w, up_b, down_w, down_b) = weights
+    (
+        residual, normed_all, qkv_own, qkv, attended_own, logsum, attended, middle,
+        normed_two, pre_act, hidden,
+    ) = kept
+    width = residual.shape[-1]
+    own = width // 2
+    d_down = low(upstream)
+    grad_down_b = jnp.sum(wide(d_down), axis=0)
+    grad_down = share_of(low(t_times(hidden, d_down)), core)
+    d_hidden = times_t(d_down, down_w)
+    _, pull = jax.vjp(lambda u: jax.nn.gelu(u, approximate=False), pre_act)
+    d_pre = low(pull(d_hidden)[0])
+    grad_up_b = jnp.sum(wide(d_pre), axis=0)
+    grad_up = share_of(low(t_times(normed_two, d_pre)), core)
+    d_normed_two = times_t(d_pre, up_w)
+    d_middle, grad_g2, grad_b2 = norm_backward(middle, wide(g2), d_normed_two)
+    d_middle = d_middle + upstream
+    d_branch = low(d_middle)
+    grad_out_b = jnp.sum(wide(d_branch), axis=0)
+    grad_out = share_of(low(t_times(attended, d_branch)), core)
+    d_attended = low(times_t(d_branch, out_w))
+    received = to_partner(half(d_attended, 1 - core, 1))
+    d_attended_own = join(half(d_attended, core, 1), received, core, 0)
+    d_qkv, bias_sums = attention_backward(
+        qkv, attended_own, d_attended_own, logsum, segments, ranges, width // head_count
+    )
+    bias_sums = bias_sums[0]
+    nothing = jnp.zeros((own,), jnp.float32)
+    grad_q_b = join(bias_sums[:own], nothing, core, 0)
+    grad_v_b = join(bias_sums[2 * own :], nothing, core, 0)
+    partial = times_t(d_qkv, qkv_own)
+    other = to_partner(low(half(partial, 1 - core, 0)))
+    d_normed = half(partial, core, 0) + wide(other)
+    grad_qkv = head_share_of(low(t_times(normed_all, d_qkv)), core)
+    d_residual, grad_g1, grad_b1 = norm_backward(residual, wide(g1), d_normed)
+    small = (grad_g1, grad_b1, grad_q_b, grad_v_b, grad_out_b, grad_g2, grad_b2, grad_up_b, grad_down_b)
+    return d_residual + d_middle, (grad_qkv, grad_out, grad_up, grad_down), small
+
+
+def core_rows(grad, core):
+    count = lax.axis_size("dp") // 2
+    rows = grad.shape[0] // (2 * count)
+    split = grad.reshape(count, 2, rows, grad.shape[1])
+    keep = lax.dynamic_index_in_dim(split, core, axis=1, keepdims=False)
+    send = lax.dynamic_index_in_dim(split, 1 - core, axis=1, keepdims=False)
+    return keep, to_partner(send)
+
+
+def reduce_chips(total):
+    size = lax.axis_size("dp")
+    groups = [list(range(0, size, 2)), list(range(1, size, 2))]
+    share = lax.psum_scatter(
+        total.reshape(-1, total.shape[-1]), "dp", scatter_dimension=0,
+        axis_index_groups=groups, tiled=True,
+    )
+    return wide(share) + wide(lax.ppermute(share, "blk", [(0, 1), (1, 0)]))
+
+
+def share_of(grad, core):
+    keep, got = core_rows(grad, core)
+    return reduce_chips(low(wide(keep) + wide(got)))
+
+
+def head_share_of(grad, core):
+    keep, got = core_rows(grad, core)
+    shape = keep.shape[:2] + (3, 1, keep.shape[2] // 3)
+    total = join(keep.reshape(shape), got.reshape(shape), core, 3)
+    return reduce_chips(total.reshape(keep.shape[:2] + (-1,)))
+
+
+def small_shares(small):
+    size = lax.axis_size("dp")
+    packed = jnp.concatenate([grad.reshape(size, -1) for grad in small], axis=1)
+    total = lax.psum(packed, ("dp", "blk"))
+    mine = lax.dynamic_index_in_dim(total, lax.axis_index("dp"), axis=0, keepdims=False)
+    shares, at = [], 0
+    for grad in small:
+        length = grad.shape[0] // size
+        shares.append(mine[at : at + length])
+        at = at + length
+    return shares
+
+
+def ordered(large, small):
+    qkv, out, up, down = large
+    g1, b1, q_b, v_b, out_b, g2, b2, up_b, down_b = small
+    return (g1, b1, qkv, q_b, v_b, out, out_b, g2, b2, up, up_b, down, down_b)
+
+
+def chip_device(patches, vis_slot, seg_ids, *rest):
+    enc_weights, (emb_weight, emb_bias, mask_token) = rest[0:13], rest[13:16]
+    dec_weights, cotangent = rest[16:29], rest[29]
+    core = lax.axis_index("dp") % 2
+    span, visible = seg_ids.shape[1], vis_slot.shape[1]
+    marks = relocate(jnp.concatenate([seg_ids[0], vis_slot[0]]))
+    rows = relocate(patches[0])
+    seg_here, slots = marks[:span], marks[span:]
+    chosen = slots[None, :] == lax.broadcasted_iota(jnp.int32, (span, visible), 0)
+    vis_here = jnp.sum(jnp.where(chosen, seg_here[:, None], 0), axis=0)
+    both = jnp.concatenate([seg_here, vis_here])
+    across = to_partner(both)
+    segments = join(both[:span], across[:span], core, 0)
+    vis_segments = join(both[span:], across[span:], core, 0)
+    ranges = key_ranges(segments, 2 * span)
+    vis_ranges = key_ranges(vis_segments, 2 * visible)
+
+    residual = wide(rows)
+    encoded, enc_kept = strip_forward(
+        residual, vis_segments, vis_ranges, enc_weights, HEADS_ENC, core
+    )
+    upstream, encoded = lax.optimization_barrier((cotangent[0], encoded))
+    upstream = relocate(upstream)
+    encoded_low = low(encoded)
+    onehot = chosen.astype(jnp.bfloat16)
+    placed = low(times(onehot, encoded_low))
+    shown = jnp.sum(onehot.astype(jnp.float32), axis=1, keepdims=True)
+    dec_in = (
+        times(placed, emb_weight) + shown * wide(emb_bias) + (1.0 - shown) * wide(mask_token)
+    )
+    decoded, dec_kept = strip_forward(dec_in, segments, ranges, dec_weights, HEADS_DEC, core)
+    dec_out = relocate(low(decoded))
+    d_dec_in, dec_large, dec_small = strip_backward(
+        wide(upstream), dec_kept, dec_weights, segments, ranges, HEADS_DEC, core
+    )
+    grad_emb_bias = jnp.sum(d_dec_in * shown, axis=0)
+    grad_mask = jnp.sum(d_dec_in * (1.0 - shown), axis=0)
+    d_shown = low(t_times(onehot, low(d_dec_in)))
+    grad_emb = share_of(low(t_times(encoded_low, d_shown)), core)
+    d_encoded = times_t(d_shown, emb_weight)
+    d_rows, enc_large, enc_small = strip_backward(
+        d_encoded, enc_kept, enc_weights, vis_segments, vis_ranges, HEADS_ENC, core
+    )
+    grad_patches = relocate(low(d_rows))
+    dec_shares = small_shares(dec_small + (grad_emb_bias, grad_mask))
+    enc_shares = small_shares(enc_small)
+    return (
+        (dec_out[None], grad_patches[None])
+        + ordered(enc_large, enc_shares)
+        + (grad_emb, dec_shares[9], dec_shares[10])
+        + ordered(dec_large, dec_shares[:9])
+    )
+
+
 def solution(mesh):
+    one_strip_a_core = mesh.shape["blk"] == 2
     return jax.shard_map(
-        per_device,
+        chip_device if one_strip_a_core else per_device,
         mesh=mesh,
         in_specs=(
             P("dp", "blk", None),

time: 1610 us -> 901 us (0.56)
  blocking collectives: 689 us -> 0 us
  waiting for transfers between devices: 37.7 us -> 423 us
  local copies, waits for them, and re-layouts: 375 us -> 78.8 us
  matrix products: 374 us -> 115 us
  Pallas kernels: 0 us -> 148 us
  other arithmetic: 107 us -> 65.2 us
  starting transfers between devices: 0.78 us -> 41.3 us
    unnamed x2 -> x0, blocking collectives: 683 us -> none
    reduce_scatter x2 -> x9, waiting for transfers between devices: 0.01 us -> 386 us  [reduce_chips(): lax.psum_scatter(total.reshape(-1, total.shape[-1]), 'dp', scatter_dimens...]
    dot_general x39 -> x28, matrix products: 374 us -> 115 us  [the longest x9 45.5 us: times(): return jnp.dot(left, right, preferred_element_type=jnp.float32)]
    unnamed x228 -> x180, local copies, waits for them, and re-layouts: 212 us -> 23.7 us
    pallas_call x0 -> x4, Pallas kernels: none -> 148 us  [the longest x2 78 us: attention_backward(): pl.pallas_call(functools.partial(attention_backward_kernel, rows, head_si...]
    reshape x39 -> x25, local copies, waits for them, and re-layouts: 124 us -> 14 us  [the longest x4 10.7 us: head_share_of(): total = join(keep.reshape(shape), got.reshape(shape), core, 3)]
    reduce_sum x16 -> x9, other arithmetic: 63.6 us -> 10.4 us  [the longest x2 6.74 us: norm_backward(): jnp.sum(upstream * normal, axis=0)]
    ppermute x0 -> x32, starting transfers between devices: none -> 40.5 us  [the longest x18 15.9 us: to_partner(): return lax.ppermute(values, 'dp', pairs(lax.axis_size('dp')))]
  transfers between devices with their start and end apart: 9 -> 42, of which waited for: 3 -> 15; matrix products, arithmetic and copies ran while one was open for 20% -> 20% of each run, Pallas kernels for 0% -> 9%
where the time goes in v1:
time: 901 us; the launch traced here: 888 us
  waiting for transfers between devices  423 us (47%)
  Pallas kernels  148 us (16%)
  matrix products  115 us (13%)
  local copies, waits for them, and re-layouts  78.8 us (9%)
  other arithmetic  65.2 us (7%)
  starting transfers between devices  41.3 us (5%)
  between operations  17.3 us (2%)
    reduce_scatter x9, waiting for transfers between devices, reduce_chips(): lax.psum_scatter(total.reshape(-1, total.shape[-1]), 'dp', scatter_dimens...  386 us
    pallas_call x2, Pallas kernels, attention_backward(): pl.pallas_call(functools.partial(attention_backward_kernel, rows, head_si...  78 us
    pallas_call x2, Pallas kernels, attention_forward(): pl.pallas_call(functools.partial(attention_forward_kernel, rows, head_siz...  70.1 us
    dot_general x9, matrix products, times(): return jnp.dot(left, right, preferred_element_type=jnp.float32)  45.5 us
    dot_general x9, matrix products, times_t(): return lax.dot_general(left, right, NT, preferred_element_type=jnp.float32)  40.4 us
    dot_general x10, matrix products, t_times(): lax.dot_general(left, right, (((0,), (0,)), ((), ())), preferred_element_...  28.6 us
    unnamed x180, local copies, waits for them, and re-layouts  23.7 us
    convert_element_type x11, other arithmetic, low(): return values.astype(jnp.bfloat16)  22.7 us
  transfers between devices with their start and end apart: 42, of which 15 were waited for; matrix products, arithmetic and copies ran while one was open for 20% of the time, Pallas kernels for 9%

profile of v1, /device:TPU:0, one launch (start us, length us, event | category | flops | bytes accessed | tf_op | source)
XLA Modules:
  0.0 888.3 jit_solution(4656805061641735329)
XLA Ops:
  13.7 5.8 copy.94
  42.4 27.1 %attention_forward.2 = (bf16[1024,384]{1,0:T(8,128)(2,1)}, f32[1024,384]{1,0:T(8,128)}) custom-call(s32[8]{0:T(128)} %pad_add_fusion.4.ranges, bf16[1024,1152]{1,0:T(8,128)(2,1)} %multiply_convert_fusion.2.q_ref.k_ref.v_ref, bf16[1024,1152]{1,0:T(8,128)(2,1)} %multiply_convert_fusion.2.q_ref.k_ref.v_ref, ...), custom_call_target="tpu_custom_call" | custom-call | tf_op jit(solution)/shard_map/attention_forward/pallas_call | solution.py:110
  76.5 19.8 %multiply_convert_fusion = (bf16[512,3072]{1,0:T(8,128)(2,1)S(1)}, f32[512,3072]{1,0:T(8,128)}, f32[512,3072]{1,0:T(8,128)}) fusion(f32[3072]{0:T(1024)S(1)} %convert_element_type.358, bf16[768,3072]{1,0:T(8,128)(2,1)} %param.45, f32[512,768]{1,0:T(8,128)S(1)} %get-tuple-element.136, f32[768]{0:T(1024)S(1)} %convert_element_type.356, ...), kind=kOutput, calls=%fused_computation.5 | convolution fusion | flops 2521694208 | bytes 22042624 | tf_op jit(solution)/shard_map/dot_general | solution.py:783
  112.7 43.0 %attention_forward.3 = (bf16[1344,256]{1,0:T(8,128)(2,1)}, f32[1344,256]{1,0:T(8,128)}) custom-call(s32[12]{0:T(128)} %pad_add_fusion.5.ranges, bf16[1344,768]{1,0:T(8,128)(2,1)} %multiply_convert_fusion.3.q_ref.k_ref.v_ref, bf16[1344,768]{1,0:T(8,128)(2,1)} %multiply_convert_fusion.3.q_ref.k_ref.v_ref, ...), custom_call_target="tpu_custom_call" | custom-call | tf_op jit(solution)/shard_map/attention_forward/pallas_call | solution.py:110
  164.1 16.2 %convert_reduce_fusion.1 = (f32[2048]{0:T(1024)}, bf16[672,2048]{1,0:T(8,128)(2,1)S(1)}, f32[672,2048]{1,0:T(8,128)}) fusion(f32[672,2048]{1,0:T(8,128)S(1)} %fusion.68, f32[2048]{0:T(1024)S(1)} %convert_element_type.379, bf16[672,512]{1,0:T(8,128)(2,1)S(1)} %collective-permute-done.8, bf16[2048,512]{1,0:T(8,128)(2,1)S(1)} %copy-done), kind=kOutput, calls=%fused_computation.20 | convolution fusion | flops 1512503296 | bytes 16564224 | tf_op jit(solution)/shard_map/dot_general | solution.py:787
  185.4 6.7 collective-permute-start.9
  198.7 47.1 %attention_backward.2 = (bf16[1344,768]{1,0:T(8,128)(2,1)}, f32[8,768]{1,0:T(8,128)}) custom-call(s32[12]{0:T(128)} %pad_add_fusion.5.ranges, bf16[1344,768]{1,0:T(8,128)(2,1)} %multiply_convert_fusion.3.q_ref.k_ref.v_ref, bf16[1344,768]{1,0:T(8,128)(2,1)} %multiply_convert_fusion.3.q_ref.k_ref.v_ref, ...), custom_call_target="tpu_custom_call" | custom-call | tf_op jit(solution)/shard_map/attention_backward/pallas_call | solution.py:280
  267.4 9.1 %convert_reduce_fusion = (f32[3072]{0:T(1024)S(1)}, bf16[512,3072]{1,0:T(8,128)(2,1)S(1)}) fusion(f32[512,3072]{1,0:T(8,128)} %get-tuple-element.94, bf16[3072,768]{1,0:T(8,128)(2,1)} %param.47, f32[512,768]{1,0:T(8,128)S(1)} %fusion.78, f32[512,3072]{1,0:T(8,128)} %get-tuple-element.137, f32[3072]{0:T(1024)S(1)} %copy-done.47), kind=kOutput, calls=%fused_computation.3 | convolution fusion | flops 2443047936 | bytes 22044672 | tf_op jit(solution)/shard_map/dot_general | solution.py:787
  286.1 30.9 %attention_backward.3 = (bf16[1024,1152]{1,0:T(8,128)(2,1)}, f32[8,1152]{1,0:T(8,128)}) custom-call(s32[8]{0:T(128)} %pad_add_fusion.4.ranges, bf16[1024,1152]{1,0:T(8,128)(2,1)} %multiply_convert_fusion.2.q_ref.k_ref.v_ref, bf16[1024,1152]{1,0:T(8,128)(2,1)} %multiply_convert_fusion.2.q_ref.k_ref.v_ref, ...), custom_call_target="tpu_custom_call" | custom-call | tf_op jit(solution)/shard_map/attention_backward/pallas_call | solution.py:280
  356.7 5.7 multiply_convert_fusion.1
  368.5 5.0 convolution_convert_fusion.2
  381.2 5.3 maximum_select_fusion
  390.5 5.1 select_n.296
  395.9 5.0 convolution_convert_fusion
  408.5 5.3 convolution_convert_fusion.1
  426.1 6.7 collective-permute-start.7
  432.9 6.8 collective-permute-done.27
  447.6 13.6 %all-reduce.12.cloned.1.call-done = (f32[16,576]{1,0:T(8,128)}, f32[16,448]{1,0:T(8,128)}) async-done(((f32[16,576]{1,0:T(8,128)}, f32[16,448]{1,0:T(8,128)}), (f32[16,576]{1,0:T(8,128)}, f32[16,448]{1,0:T(8,128)})) %all-reduce.12.cloned.1.call-update) | async-done | bytes 65552 | tf_op jit(solution)/shard_map/psum | solution.py:897
  469.7 54.1 %reduce-scatter.12.cloned.1.call-done = bf16[48,768]{1,0:T(8,128)(2,1)} async-done(((bf16[384,768]{1,0:T(8,128)(2,1)}), bf16[48,768]{1,0:T(8,128)(2,1)}) %reduce-scatter.12.cloned.1.call-update) | async-done | bytes 73744 | tf_op jit(solution)/shard_map/reduce_scatter | solution.py:875
  526.9 63.4 %reduce-scatter.24.cloned.1.call-done = bf16[32,2048]{1,0:T(8,128)(2,1)} async-done(((bf16[256,2048]{1,0:T(8,128)(2,1)}), bf16[32,2048]{1,0:T(8,128)(2,1)}) %reduce-scatter.24.cloned.1.call-update) | async-done | bytes 131088 | tf_op jit(solution)/shard_map/reduce_scatter | solution.py:875
  593.3 63.3 %reduce-scatter.26.cloned.1.call-done = bf16[128,512]{1,0:T(8,128)(2,1)} async-done(((bf16[1024,512]{1,0:T(8,128)(2,1)}), bf16[128,512]{1,0:T(8,128)(2,1)}) %reduce-scatter.26.cloned.1.call-update) | async-done | bytes 131088 | tf_op jit(solution)/shard_map/reduce_scatter | solution.py:875
  659.7 65.9 %reduce-scatter.10.cloned.1.call-done = bf16[48,2304]{1,0:T(8,128)(2,1)} async-done(((bf16[384,2304]{1,0:T(8,128)(2,1)}), bf16[48,2304]{1,0:T(8,128)(2,1)}) %reduce-scatter.10.cloned.1.call-update) | async-done | bytes 221200 | tf_op jit(solution)/shard_map/reduce_scatter | solution.py:875
  728.7 68.8 %reduce-scatter.16.cloned.1.call-done = bf16[192,768]{1,0:T(8,128)(2,1)} async-done(((bf16[1536,768]{1,0:T(8,128)(2,1)}), bf16[192,768]{1,0:T(8,128)(2,1)}) %reduce-scatter.16.cloned.1.call-update) | async-done | bytes 294928 | tf_op jit(solution)/shard_map/reduce_scatter | solution.py:875
  799.0 70.8 %reduce-scatter.14.cloned.1.call-done = bf16[48,3072]{1,0:T(8,128)(2,1)} async-done(((bf16[384,3072]{1,0:T(8,128)(2,1)}), bf16[48,3072]{1,0:T(8,128)(2,1)}) %reduce-scatter.14.cloned.1.call-update) | async-done | bytes 294928 | tf_op jit(solution)/shard_map/reduce_scatter | solution.py:875
  (444 shorter events, 220.5 us)
Async XLA Ops:
  8.1 424.8 %reduce-scatter.22.cloned.1.call-start = ((), (), s32[]{:S(2)}) async-start(), calls=%async_computation.15 | async-start | bytes 294912 | tf_op jit(solution)/shard_map/reduce_scatter | solution.py:875
  8.1 26.3 %collective-permute-start.1 = (bf16[512,768]{1,0:T(8,128)(2,1)}, bf16[512,768]{1,0:T(8,128)(2,1)S(1)}, u32[]{:S(2)}, u32[]{:S(2)}) collective-permute-start(bf16[512,768]{1,0:T(8,128)(2,1)} %bitcast.200), channel_id=1, source_target_pairs={{0,0},{1,2},{2,1},{3,3},{4,4},{5,6},{6,5},{7,7},{8,8},{9,10},{10,9... | collective-permute-start | bytes 2359304 | tf_op jit(solution)/shard_map/ppermute | solution.py:733
  11.5 14.5 %collective-permute-start = (s32[1184]{0:T(1024)S(1)}, s32[1184]{0:T(1024)S(1)}, u32[]{:S(2)}, u32[]{:S(2)}) collective-permute-start(s32[1184]{0:T(1024)S(1)} %pad_add_fusion), channel_id=1, source_target_pairs={{0,0},{1,2},{2,1},{3,3},{4,4},{5,6},{6,5},{7,7},{8,8},{9,10},{10,9... | collective-permute-start | bytes 14216 | tf_op jit(solution)/shard_map/ppermute | solution.py:733
  185.4 11.0 %collective-permute-start.9 = (bf16[672,256]{1,0:T(8,128)(2,1)}, bf16[672,256]{1,0:T(8,128)(2,1)}, u32[]{:S(2)}, u32[]{:S(2)}) collective-permute-start(bf16[672,256]{1,0:T(8,128)(2,1)} %get-tuple-element.108), channel_id=1, source_target_pairs={{0,2},{2,0},{4,6},{6,4},{8,10},{10,8},{12,14},{14,12},{16,18},{18,... | collective-permute-start | bytes 1032200 | tf_op jit(solution)/shard_map/ppermute | solution.py:725
  195.4 56.5 %collective-permute-start.26 = (bf16[8,32,512]{2,1,0:T(8,128)(2,1)}, bf16[8,32,512]{2,1,0:T(8,128)(2,1)}, u32[]{:S(2)}, u32[]{:S(2)}) collective-permute-start(bf16[8,32,512]{2,1,0:T(8,128)(2,1)} %dynamic-slice_bitcast_fusion.10), channel_id=1, source_target_pairs={{0,2},{2,0},{4,6},{6,4},{8,10},{10,8},{12,14},{14,12},{16,18},{18,... | collective-permute-start | bytes 786440 | tf_op jit(solution)/shard_map/ppermute | solution.py:725
  253.6 192.6 %reduce-scatter.18.cloned.1.call-start = ((), (), s32[]{:S(2)}) async-start(), calls=%async_computation.13 | async-start | bytes 442368 | tf_op jit(solution)/shard_map/reduce_scatter | solution.py:875
  258.5 67.9 %collective-permute-start.24 = (bf16[8,32,768]{2,1,0:T(8,128)(2,1)}, bf16[8,32,768]{2,1,0:T(8,128)(2,1)}, u32[]{:S(2)}, u32[]{:S(2)}) collective-permute-start(bf16[8,32,768]{2,1,0:T(8,128)(2,1)} %get-tuple-element.101), channel_id=1, source_target_pairs={{0,2},{2,0},{4,6},{6,4},{8,10},{10,8},{12,14},{14,12},{16,18},{18,... | collective-permute-start | bytes 1179656 | tf_op jit(solution)/shard_map/ppermute | solution.py:725
  284.8 39.8 %collective-permute-start.22 = (bf16[8,48,512]{2,1,0:T(8,128)(2,1)}, bf16[8,48,512]{2,1,0:T(8,128)(2,1)S(1)}, u32[]{:S(2)}, u32[]{:S(2)}) collective-permute-start(bf16[8,48,512]{2,1,0:T(8,128)(2,1)} %dynamic-slice_bitcast_fusion.9), channel_id=1, source_target_pairs={{0,2},{2,0},{4,6},{6,4},{8,10},{10,8},{12,14},{14,12},{16,18},{18,... | collective-permute-start | bytes 1179656 | tf_op jit(solution)/shard_map/ppermute | solution.py:725
  325.5 135.7 %all-reduce.12.cloned.1.call-start = ((), (), s32[]{:S(2)}) async-start(), calls=%async_computation.18 | async-start | bytes 147456 | tf_op jit(solution)/shard_map/psum | solution.py:897
  335.5 131.3 %reduce-scatter.20.cloned.1.call-start = ((), (), s32[]{:S(2)}) async-start(), calls=%async_computation.14 | async-start | bytes 884736 | tf_op jit(solution)/shard_map/reduce_scatter | solution.py:875
  343.1 180.7 %reduce-scatter.12.cloned.1.call-start = ((), (), s32[]{:S(2)}) async-start(), calls=%async_computation.10 | async-start | bytes 663552 | tf_op jit(solution)/shard_map/reduce_scatter | solution.py:875
  351.8 238.4 %reduce-scatter.24.cloned.1.call-start = ((), (), s32[]{:S(2)}) async-start(), calls=%async_computation.16 | async-start | bytes 1179648 | tf_op jit(solution)/shard_map/reduce_scatter | solution.py:875
  356.4 300.2 %reduce-scatter.26.cloned.1.call-start = ((), (), s32[]{:S(2)}) async-start(), calls=%async_computation.17 | async-start | bytes 1179648 | tf_op jit(solution)/shard_map/reduce_scatter | solution.py:875
  368.4 357.2 %reduce-scatter.10.cloned.1.call-start = ((), (), s32[]{:S(2)}) async-start(), calls=%async_computation.9 | async-start | bytes 1990656 | tf_op jit(solution)/shard_map/reduce_scatter | solution.py:875
  395.6 402.0 %reduce-scatter.16.cloned.1.call-start = ((), (), s32[]{:S(2)}) async-start(), calls=%async_computation.12 | async-start | bytes 2654208 | tf_op jit(solution)/shard_map/reduce_scatter | solution.py:875
  407.8 462.0 %reduce-scatter.14.cloned.1.call-start = ((), (), s32[]{:S(2)}) async-start(), calls=%async_computation.11 | async-start | bytes 2654208 | tf_op jit(solution)/shard_map/reduce_scatter | solution.py:875
  444.4 148.9 %collective-permute-start.13 = (bf16[512,768]{1,0:T(8,128)(2,1)}, bf16[512,768]{1,0:T(8,128)(2,1)S(1)}, u32[]{:S(2)}, u32[]{:S(2)}) collective-permute-start(bf16[512,768]{1,0:T(8,128)(2,1)} %fusion.28), channel_id=1, source_target_pairs={{0,0},{1,2},{2,1},{3,3},{4,4},{5,6},{6,5},{7,7},{8,8},{9,10},{10,9... | collective-permute-start | bytes 2359304 | tf_op jit(solution)/shard_map/ppermute | solution.py:733
  446.2 22.0 %collective-permute-start.23 = (bf16[48,512]{1,0:T(8,128)(2,1)}, bf16[48,512]{1,0:T(8,128)(2,1)S(1)}, u32[]{:S(2)}, u32[]{:S(2)}) collective-permute-start(bf16[48,512]{1,0:T(8,128)(2,1)} %reduce-scatter.18.cloned.1.call-done), channel_id=1, source_target_pairs={{0,1},{1,0},{2,3},{3,2},{4,5},{5,4},{6,7},{7,6},{8,9},{9,8},{10,11... | collective-permute-start | bytes 147464 | tf_op jit(solution)/shard_map/ppermute | solution.py:879
  466.8 58.5 %collective-permute-start.25 = (bf16[32,1536]{1,0:T(8,128)(2,1)}, bf16[32,1536]{1,0:T(8,128)(2,1)S(1)}, u32[]{:S(2)}, u32[]{:S(2)}) collective-permute-start(bf16[32,1536]{1,0:T(8,128)(2,1)} %reduce-scatter.20.cloned.1.call-done), channel_id=1, source_target_pairs={{0,1},{1,0},{2,3},{3,2},{4,5},{5,4},{6,7},{7,6},{8,9},{9,8},{10,11... | collective-permute-start | bytes 294920 | tf_op jit(solution)/shard_map/ppermute | solution.py:879
  523.8 67.9 %collective-permute-start.17 = (bf16[48,768]{1,0:T(8,128)(2,1)}, bf16[48,768]{1,0:T(8,128)(2,1)S(1)}, u32[]{:S(2)}, u32[]{:S(2)}) collective-permute-start(bf16[48,768]{1,0:T(8,128)(2,1)} %reduce-scatter.12.cloned.1.call-done), channel_id=1, source_target_pairs={{0,1},{1,0},{2,3},{3,2},{4,5},{5,4},{6,7},{7,6},{8,9},{9,8},{10,11... | collective-permute-start | bytes 221192 | tf_op jit(solution)/shard_map/ppermute | solution.py:879
  590.2 67.8 %collective-permute-start.29 = (bf16[32,2048]{1,0:T(8,128)(2,1)}, bf16[32,2048]{1,0:T(8,128)(2,1)S(1)}, u32[]{:S(2)}, u32[]{:S(2)}) collective-permute-start(bf16[32,2048]{1,0:T(8,128)(2,1)} %reduce-scatter.24.cloned.1.call-done), channel_id=1, source_target_pairs={{0,1},{1,0},{2,3},{3,2},{4,5},{5,4},{6,7},{7,6},{8,9},{9,8},{10,11... | collective-permute-start | bytes 393224 | tf_op jit(solution)/shard_map/ppermute | solution.py:879
  656.6 70.5 %collective-permute-start.31 = (bf16[128,512]{1,0:T(8,128)(2,1)}, bf16[128,512]{1,0:T(8,128)(2,1)S(1)}, u32[]{:S(2)}, u32[]{:S(2)}) collective-permute-start(bf16[128,512]{1,0:T(8,128)(2,1)} %reduce-scatter.26.cloned.1.call-done), channel_id=1, source_target_pairs={{0,1},{1,0},{2,3},{3,2},{4,5},{5,4},{6,7},{7,6},{8,9},{9,8},{10,11... | collective-permute-start | bytes 393224 | tf_op jit(solution)/shard_map/ppermute | solution.py:879
  725.6 145.7 %collective-permute-start.15 = (bf16[48,2304]{1,0:T(8,128)(2,1)}, bf16[48,2304]{1,0:T(8,128)(2,1)S(1)}, u32[]{:S(2)}, u32[]{:S(2)}) collective-permute-start(bf16[48,2304]{1,0:T(8,128)(2,1)} %reduce-scatter.10.cloned.1.call-done), channel_id=1, source_target_pairs={{0,1},{1,0},{2,3},{3,2},{4,5},{5,4},{6,7},{7,6},{8,9},{9,8},{10,11... | collective-permute-start | bytes 663560 | tf_op jit(solution)/shard_map/ppermute | solution.py:879
  797.5 75.5 %collective-permute-start.21 = (bf16[192,768]{1,0:T(8,128)(2,1)}, bf16[192,768]{1,0:T(8,128)(2,1)S(1)}, u32[]{:S(2)}, u32[]{:S(2)}) collective-permute-start(bf16[192,768]{1,0:T(8,128)(2,1)} %reduce-scatter.16.cloned.1.call-done), channel_id=1, source_target_pairs={{0,1},{1,0},{2,3},{3,2},{4,5},{5,4},{6,7},{7,6},{8,9},{9,8},{10,11... | collective-permute-start | bytes 884744 | tf_op jit(solution)/shard_map/ppermute | solution.py:879
  (106 other events, 1246.3 us)
Sparse Core Ops, SparseCore 0:
  253.8 63.5 reduce-scatter.21
  325.6 66.9 reduce-scatter.17
  395.9 62.3 reduce-scatter.19
  462.0 61.7 reduce-scatter.11
  527.0 63.1 reduce-scatter.23
  593.5 63.0 reduce-scatter.25
  660.0 65.5 reduce-scatter.9
  729.1 68.3 reduce-scatter.15
  801.0 68.7 reduce-scatter.13
Sparse Core Ops, SparseCore 1:
  335.5 125.6 all-reduce.11
